TPU v7x, 32 devices: a whole 2x2x4 slice. The times are simulated.
32 devices in a mesh: dp: 8 (over z, x), mp: 4 (over y, core).
Axes of the slice: x: 2, y: 2, z: 4, core: 2. Of those that a mesh axis runs over, the one named last changes fastest.
Arguments:
- acts: bfloat16 [1, 16384, 4096], P(None, 'dp'), may hold values from -64 to 64
- out_grads: bfloat16 [1, 16384, 4096], P(None, 'dp', 'mp'), may hold values from -80 to 80
- clip_bound: float32 [1], replicated, may hold values from 163840 to 491520
- noise: float32 [1, 4096, 4096], P(None, 'dp', 'mp'), may hold values from -6 to 6
Outputs:
- update: float32 [1, 4096, 4096], P(None, 'dp', 'mp')
All inputs are finite; a program needn't handle non-finite values.
Results may differ from a plain program's by a relative error of at most 0.0017.
Values may be sent and summed in bfloat16 or wider, within the bound.
A program may use at most 128 MiB of HBM per device.

v0:
```python
import math

import jax
import jax.numpy as jnp
from jax import lax
from jax.sharding import PartitionSpec as P

SEQ = 512


def ghost_partial(act_block, grad_block, examples):
    act_seq = act_block.reshape(examples, SEQ, act_block.shape[1])
    grad_seq = grad_block.reshape(examples, SEQ, grad_block.shape[1])
    gram_act = jnp.einsum("etd,esd->ets", act_seq, act_seq, preferred_element_type=jnp.float32)
    gram_grad = jnp.einsum("etd,esd->ets", grad_seq, grad_seq, preferred_element_type=jnp.float32)
    return jnp.sum(gram_act * gram_grad, axis=(1, 2))


def scale_grads(grad_block, norm_sq, bound, examples):
    clip = jnp.minimum(1.0, bound / jnp.sqrt(norm_sq + 1e-06))
    factor = clip / bound
    grad_seq = grad_block.reshape(examples, SEQ, grad_block.shape[1]).astype(jnp.float32)
    scaled = (grad_seq * factor[:, None, None]).astype(jnp.bfloat16)
    return scaled.reshape(grad_block.shape)


def on_device(acts, out_grads, clip_bound, noise):
    examples = acts.shape[1] // SEQ
    model_width = acts.shape[2]
    batch_total = examples * lax.axis_size("dp")
    out_factor = model_width / math.sqrt(batch_total)
    act_block = acts[0]
    norm_sq = lax.psum(ghost_partial(act_block, out_grads[0], examples), "mp")
    scaled = scale_grads(out_grads[0], norm_sq, clip_bound[0], examples)

    def term_rows(begin_row, row_count, act_block=act_block, scaled=scaled):
        return lax.dot_general(
            act_block, scaled, (((0,), (0,)), ((), ())), preferred_element_type=jnp.float32
        )

    summed = lax.psum_scatter(
        term_rows(jnp.int32(0), model_width // lax.axis_size("dp") * lax.axis_size("dp")),
        "dp",
        scatter_dimension=0,
        tiled=True,
    )
    updates = [summed * out_factor + noise[0]]
    return jnp.stack(updates)


def solution(mesh):
    placed = (P(None, "dp", None), P(None, "dp", "mp"), P(), P(None, "dp", "mp"))
    return jax.shard_map(
        on_device, mesh=mesh, in_specs=placed, out_specs=P(None, "dp", "mp"), check_vma=False
    )
```

profile of v0, /device:TPU:0, one launch (start us, length us, event | category | flops | bytes accessed | tf_op | source)
XLA Modules:
  0.0 358.5 jit_solution(12628637458226172755)
XLA Ops:
  6.5 0.0 reduce-scatter.2.cloned.1.call-start
  6.5 7.8 %fusion.9 = f32[4,512,512]{2,1,0:T(8,128)} fusion(bf16[4,512,1024]{2,1,0:T(8,128)(2,1)} %bitcast.29), kind=kOutput, calls=%fused_computation.11 | convolution fusion | flops 2147483648 | bytes 8388608 | tf_op jit(solution)/shard_map/etd,esd->ets/dot_general | solution.py:15
  14.3 16.9 %multiply_reduce_fusion = f32[4]{0:T(128)S(1)} fusion(f32[4,512,512]{2,1,0:T(8,128)} %fusion.9, bf16[4,512,4096]{2,1,0:T(8,128)(2,1)} %bitcast.28), kind=kOutput, calls=%fused_computation.6 | convolution fusion | flops 8592031744 | bytes 20971536 | tf_op jit(solution)/shard_map/etd,esd->ets/dot_general | solution.py:14
  31.2 8.6 %psum.7 = f32[4]{0:T(128)S(1)} all-reduce(f32[4]{0:T(128)S(1)} %multiply_reduce_fusion), channel_id=1, replica_groups=mesh['dp'=8,'mp'=4] {'mp'}, use_global_device_ids=true, to_apply=%region_1.0 | all-reduce | flops 4 | bytes 32 | tf_op jit(solution)/shard_map/psum | solution.py:33
  40.4 0.1 broadcast_bitcast_fusion
  40.5 24.2 %fusion.2 = f32[4096,1024]{0,1:T(8,128)} fusion(bf16[1,2048,4096]{2,1,0:T(8,128)(2,1)} %param.4, bf16[1,2048,1024]{2,1,0:T(8,128)(2,1)} %param.5, f32[2048]{0:T(1024)S(1)} %bitcast.27), kind=kOutput, calls=%fused_computation.2 | convolution fusion | flops 17186160640 | bytes 37756928 | tf_op jit(solution)/shard_map/dot_general | solution.py:37
  64.7 0.0 reduce-scatter.2.cloned.1.call-update
  64.7 1.9 copy.5
  66.7 278.7 %reduce-scatter.2.cloned.1.call-done = f32[512,1024]{0,1:T(8,128)} async-done(((f32[4096,1024]{0,1:T(8,128)}), f32[512,1024]{0,1:T(8,128)}) %reduce-scatter.2.cloned.1.call-update) | async-done | bytes 2097168 | tf_op jit(solution)/shard_map/reduce_scatter | solution.py:41
  345.4 3.4 fusion.8
  348.8 2.9 copy.6
  (2 shorter events, 0.0 us)
Async XLA Ops:
  6.5 338.8 %reduce-scatter.2.cloned.1.call-start = ((), (), s32[]{:S(2)}) async-start(), calls=%async_computation.1 | async-start | bytes 18874368 | tf_op jit(solution)/shard_map/reduce_scatter | solution.py:41
Sparse Core Ops, SparseCore 0:
  64.9 280.4 reduce-scatter.1
where the time goes:
time: 359 us
  waiting for transfers between devices  279 us (78%)
  matrix products  48.9 us (14%)
  between operations  14.1 us (4%)
  blocking collectives  8.55 us (2%)
  local copies, waits for them, and re-layouts  4.88 us (1%)
    reduce_scatter x1, waiting for transfers between devices, on_device(): lax.psum_scatter(term_rows(jnp.int32(0), model_width // lax.axis_size('dp...  279 us
    dot_general x1, matrix products, term_rows(): lax.dot_general(act_block, scaled, (((0,), (0,)), ((), ())), preferred_el...  24.2 us
    dot_general x1, matrix products, ghost_partial(): jnp.einsum('etd,esd->ets', act_seq, act_seq, preferred_element_type=jnp.f...  16.9 us
    psum x1, blocking collectives, on_device(): norm_sq = lax.psum(ghost_partial(act_block, out_grads[0], examples), 'mp')  8.55 us
    dot_general x1, matrix products, ghost_partial(): jnp.einsum('etd,esd->ets', grad_seq, grad_seq, preferred_element_type=jnp...  7.76 us
  transfers between devices with their start and end apart: 1, of which 1 were waited for; matrix products, arithmetic and copies ran while one was open for 1% of the time, Pallas kernels for 0%

commit v1 on v0

v1 whole, which is shorter than its diff:
```python
import functools
import math

import jax
import jax.numpy as jnp
from jax import lax
from jax.experimental import pallas as pl
from jax.experimental.pallas import tpu as pltpu
from jax.sharding import PartitionSpec as P

SEQ = 512
NT = (((1,), (1,)), ((), ()))
MESH = pl.DeviceIdType.MESH
LIFT = 2.0**50


def coded(value):
    lifted = value * LIFT
    return (lifted * jnp.abs(lifted)).astype(jnp.bfloat16)


def decoded(code):
    code = code.astype(jnp.float32)
    return code * lax.rsqrt(jnp.maximum(jnp.abs(code), 1e-37)) * (1.0 / LIFT)


def kernel(
    groups, lanes, acts_hbm, grads_hbm, bound_ref, out_hbm,
    acts, grads, grads_t, xs, xr, zs, zr, norm_mine, norm_peer, total, out,
    load_sem, out_sem, norm_send, norm_recv, x_send, x_recv, z_send, z_recv,
):
    planes = groups // 2
    steps = 2 * planes
    feats = acts.shape[1] // groups
    half_cols = grads.shape[1] // 2
    examples = acts.shape[0] // SEQ
    me = lax.axis_index("dp")
    lane = lax.axis_index("mp")
    line, pair = me // 2, me % 2
    has_below = (line > 0).astype(jnp.int32)
    has_above = (line < planes - 1).astype(jnp.int32)
    x_peer = {"dp": line * 2 + 1 - pair}
    above = {"dp": jnp.minimum(line + 1, planes - 1) * 2 + pair}
    below = {"dp": jnp.maximum(line - 1, 0) * 2 + pair}

    def rows_of(e):
        return pl.ds(pl.multiple_of(e * SEQ, SEQ), SEQ)

    def load(e, which):
        source, target = (grads_hbm, grads) if which else (acts_hbm, acts)
        return pltpu.make_async_copy(
            source.at[rows_of(e)], target.at[rows_of(e)], load_sem.at[which, e]
        )

    for e in range(examples):
        load(e, 1).start()
        load(e, 0).start()

    barrier = pltpu.get_barrier_semaphore()
    pl.semaphore_signal(barrier, inc=1, device_id=x_peer, device_id_type=MESH)
    for j in range(1, lanes):
        pl.semaphore_signal(
            barrier, inc=1, device_id={"mp": lax.rem(lane + j, lanes)}, device_id_type=MESH
        )

    @pl.when(line > 0)
    def _():
        pl.semaphore_signal(barrier, inc=1, device_id=below, device_id_type=MESH)

    @pl.when(line < planes - 1)
    def _():
        pl.semaphore_signal(barrier, inc=1, device_id=above, device_id_type=MESH)

    cut = SEQ // 2

    def gram(ref, e):
        base = pl.multiple_of(e * SEQ, SEQ)
        low, high = ref[pl.ds(base, cut), :], ref[pl.ds(base + cut, cut), :]
        dot = functools.partial(
            lax.dot_general, dimension_numbers=NT, preferred_element_type=jnp.float32
        )
        return dot(low, low), dot(low, high), dot(high, high)

    def norm_step(e, carry):
        load(e, 1).wait()
        gg = gram(grads, e)
        load(e, 0).wait()
        ga = gram(acts, e)
        prod = ga[0] * gg[0] + 2.0 * (ga[1] * gg[1]) + ga[2] * gg[2]
        norm_mine[e] = jnp.broadcast_to(jnp.sum(prod, keepdims=True), norm_mine.shape[1:])
        return carry

    lax.fori_loop(0, examples, norm_step, 0)
    pl.semaphore_wait(barrier, lanes + has_below + has_above)

    def norm_copy(j):
        return pltpu.make_async_remote_copy(
            src_ref=norm_mine, dst_ref=norm_peer.at[j - 1],
            send_sem=norm_send.at[j - 1], recv_sem=norm_recv.at[j - 1],
            device_id={"mp": lax.rem(lane + j, lanes)}, device_id_type=MESH,
        )

    for j in range(1, lanes):
        norm_copy(j).start()
    for j in range(1, lanes):
        norm_copy(j).wait()

    bound = bound_ref[0]

    def scale_step(e, carry):
        norm_sq = norm_mine[e]
        for j in range(1, lanes):
            norm_sq = norm_sq + norm_peer[j - 1, e]
        factor = (jnp.minimum(1.0, bound / jnp.sqrt(norm_sq + 1e-06)) / bound)[:1, :1]
        scaled = (grads[rows_of(e), :].astype(jnp.float32) * factor).astype(jnp.bfloat16)
        grads_t[:, rows_of(e)] = scaled.T
        return carry

    lax.fori_loop(0, examples, scale_step, 0)

    def target_of(k):
        ups = planes - 1 - line
        up_first = jnp.where(k < ups, planes - 1 - k, k - ups)
        down_first = jnp.where(k < line, k, planes - 1 - (k - line))
        ordered = jnp.where(line < planes // 2, up_first, down_first)
        return jnp.where(k == planes - 1, line, ordered)

    def term(block, half):
        cols = pl.ds(pl.multiple_of(block * feats, feats), feats)
        rows = pl.ds(pl.multiple_of(half * half_cols, half_cols), half_cols)
        return jnp.dot(grads_t[rows, :], acts[:, cols], preferred_element_type=jnp.float32)

    def x_copy(s):
        return pltpu.make_async_remote_copy(
            src_ref=xs.at[s], dst_ref=xr.at[s], send_sem=x_send.at[s], recv_sem=x_recv.at[s],
            device_id=x_peer, device_id_type=MESH,
        )

    def z_copy(s, slot, device):
        return pltpu.make_async_remote_copy(
            src_ref=zs.at[s], dst_ref=zr.at[slot], send_sem=z_send.at[s],
            recv_sem=z_recv.at[slot], device_id=device, device_id_type=MESH,
        )

    def send_step(s, carry):
        xs[s] = coded(term(target_of(s // 2) * 2 + 1 - pair, s % 2))
        x_copy(s).start()
        return carry

    lax.fori_loop(0, steps, send_step, 0)

    def add_arrival(slot):
        z_copy(0, slot, above).wait_recv()
        total[...] += decoded(zr[slot])

    def sum_step(s, carry):
        target, half = target_of(s // 2), s % 2
        slot = target * 2 + half
        own = term(target * 2 + pair, half)
        x_copy(s).wait_recv()
        total[...] = own + decoded(xr[s])

        @pl.when((target >= line) & (line > 0))
        def _():
            add_arrival(slot)

        @pl.when((target < line) & (line < planes - 1))
        def _():
            add_arrival(slot)

        @pl.when((target == line) & (line < planes - 1))
        def _():
            add_arrival(steps + half)

        @pl.when(target > line)
        def _():
            zs[s] = coded(total[...])
            z_copy(s, slot, above).start()

        @pl.when(target < line)
        def _():
            zs[s] = coded(total[...])
            z_copy(s, jnp.where(target == line - 1, steps + half, slot), below).start()

        @pl.when(target == line)
        def _():
            cols = pl.ds(pl.multiple_of(half * half_cols, half_cols), half_cols)
            out[:, cols] = total[...].T
            pltpu.make_async_copy(out.at[:, cols], out_hbm.at[:, cols], out_sem.at[half]).start()

        return carry

    lax.fori_loop(0, steps, sum_step, 0)

    def drain_step(s, carry):
        x_copy(s).wait_send()

        @pl.when(s < steps - 2)
        def _():
            z_copy(s, 0, above).wait_send()

        return carry

    lax.fori_loop(0, steps, drain_step, 0)
    for half in range(2):
        cols = pl.ds(half * half_cols, half_cols)
        pltpu.make_async_copy(out.at[:, cols], out_hbm.at[:, cols], out_sem.at[half]).wait()


def clipped_sum(act_block, grad_block, bound):
    groups, lanes = lax.axis_size("dp"), lax.axis_size("mp")
    tokens, width = act_block.shape
    cols = grad_block.shape[1]
    feats = width // groups
    steps = groups
    examples = tokens // SEQ
    half = (cols // 2, feats)
    dma = pltpu.SemaphoreType.DMA
    any_space = pl.BlockSpec(memory_space=pl.ANY)
    return pl.pallas_call(
        functools.partial(kernel, groups, lanes),
        out_shape=jax.ShapeDtypeStruct((feats, cols), jnp.float32),
        in_specs=[any_space, any_space, pl.BlockSpec(memory_space=pltpu.SMEM)],
        out_specs=any_space,
        scratch_shapes=[
            pltpu.VMEM((tokens, width), jnp.bfloat16),
            pltpu.VMEM((tokens, cols), jnp.bfloat16),
            pltpu.VMEM((cols, tokens), jnp.bfloat16),
            pltpu.VMEM((steps,) + half, jnp.bfloat16),
            pltpu.VMEM((steps,) + half, jnp.bfloat16),
            pltpu.VMEM((steps,) + half, jnp.bfloat16),
            pltpu.VMEM((steps + 2,) + half, jnp.bfloat16),
            pltpu.VMEM((examples, 8, 128), jnp.float32),
            pltpu.VMEM((max(lanes - 1, 1), examples, 8, 128), jnp.float32),
            pltpu.VMEM(half, jnp.float32),
            pltpu.VMEM((feats, cols), jnp.float32),
            dma((2, examples)),
            dma((2,)),
            dma((max(lanes - 1, 1),)),
            dma((max(lanes - 1, 1),)),
            dma((steps,)),
            dma((steps,)),
            dma((steps,)),
            dma((steps + 2,)),
        ],
        compiler_params=pltpu.CompilerParams(
            collective_id=0, has_side_effects=True, vmem_limit_bytes=60 * 2**20
        ),
        name="clipped_sum",
    )(act_block, grad_block, bound)


def on_device(acts, out_grads, clip_bound, noise):
    model_width = acts.shape[2]
    batch_total = acts.shape[1] // SEQ * lax.axis_size("dp")
    out_factor = model_width / math.sqrt(batch_total)
    updates = [
        clipped_sum(acts[g], out_grads[g], clip_bound[g : g + 1]) * out_factor + noise[g]
        for g in range(acts.shape[0])
    ]
    return jnp.stack(updates)


def solution(mesh):
    placed = (P(None, "dp", None), P(None, "dp", "mp"), P(), P(None, "dp", "mp"))
    return jax.shard_map(
        on_device, mesh=mesh, in_specs=placed, out_specs=P(None, "dp", "mp"), check_vma=False
    )
```

time: 359 us -> 123 us (0.34)
  waiting for transfers between devices: 279 us -> 0 us
  Pallas kernels: 0 us -> 118 us
  matrix products: 48.9 us -> 0 us
  between operations: 14.1 us -> 0.68 us
  blocking collectives: 8.55 us -> 0 us
  local copies, waits for them, and re-layouts: 4.88 us -> 0.01 us
    reduce_scatter x1 -> x0, waiting for transfers between devices: 279 us -> none  [on_device(): lax.psum_scatter(term_rows(jnp.int32(0), model_width // lax.axis_size('dp...]
    pallas_call x0 -> x1, Pallas kernels: none -> 118 us  [clipped_sum(): pl.pallas_call(functools.partial(kernel, groups, lanes), out_shape=jax.Sh...]
    dot_general x3 -> x0, matrix products: 48.9 us -> none  [the longest x1 24.2 us: term_rows(): lax.dot_general(act_block, scaled, (((0,), (0,)), ((), ())), preferred_el...]
    psum x1 -> x0, blocking collectives: 8.55 us -> none  [on_device(): norm_sq = lax.psum(ghost_partial(act_block, out_grads[0], examples), 'mp')]
  transfers between devices with their start and end apart: 1 -> 0, of which waited for: 1 -> 0; matrix products, arithmetic and copies ran while one was open for 1% -> 0% of each run, Pallas kernels for 0% -> 0%
where the time goes in v1:
time: 123 us
  Pallas kernels  118 us (96%)
  other arithmetic  3.53 us (3%)
    pallas_call x1, Pallas kernels, clipped_sum(): pl.pallas_call(functools.partial(kernel, groups, lanes), out_shape=jax.Sh...  118 us
    another operation x1, other arithmetic, on_device(): return jnp.stack(updates)  3.53 us

profile of v1, /device:TPU:0, one launch (start us, length us, event | category | flops | bytes accessed | tf_op | source)
XLA Modules:
  0.0 122.5 jit_solution(14583100408464639974)
XLA Ops:
  0.7 0.0 copy-start
  0.7 118.3 %clipped_sum.1 = f32[512,1024]{1,0:T(8,128)} custom-call(bf16[2048,4096]{1,0:T(8,128)(2,1)} %bitcast.8, bf16[2048,1024]{1,0:T(8,128)(2,1)} %bitcast.9, f32[1]{0:T(128)S(6)} %copy.5.bound_ref), custom_call_target="tpu_custom_call" | custom-call | tf_op jit(solution)/shard_map/clipped_sum/pallas_call | solution.py:220
  119.0 0.0 copy-done
  119.0 3.5 %fusion = f32[1,512,1024]{2,1,0:T(8,128)} fusion(f32[1,512,1024]{2,1,0:T(8,128)S(1)} %copy-done, f32[512,1024]{1,0:T(8,128)} %clipped_sum.1), kind=kLoop, calls=%fused_computation.1 | loop fusion | flops 1048576 | bytes 6291456 | tf_op jit(solution)/shard_map/stack | solution.py:261
Async XLA Ops:
  0.7 118.3 %copy-start = (f32[1,512,1024]{2,1,0:T(8,128)S(1)}, f32[1,512,1024]{2,1,0:T(8,128)}, u32[]{:S(2)}) copy-start(f32[1,512,1024]{2,1,0:T(8,128)} %param.7) | copy-start | bytes 6291460
